TPU v7x, 8 devices: a whole 2x2x1 slice. The times are simulated.
8 devices in a mesh: rep: 2 (over y, z), dp: 4 (over x, core).
Axes of the slice: x: 2, y: 2, z: 1, core: 2. Of those that a mesh axis runs over, the one named last changes fastest.
Arguments:
- x: bfloat16 [8, 2048, 1024], P(('rep', 'dp')), parts along dimension 0
- dy: bfloat16 [8, 2048, 1024], P(('rep', 'dp')), parts along dimension 0
- w_gate: bfloat16 [2, 1024, 2560], replicated
- w_up: bfloat16 [2, 1024, 2560], replicated
- w_down: bfloat16 [2, 2560, 1024], replicated
- m_w_gate: float32 [2, 1024, 2560], replicated
- m_w_up: float32 [2, 1024, 2560], replicated
- m_w_down: float32 [2, 2560, 1024], replicated
- v_w_gate: float32 [2, 1024, 2560], replicated
- v_w_up: float32 [2, 1024, 2560], replicated
- v_w_down: float32 [2, 2560, 1024], replicated
Outputs:
- output 1: bfloat16 [4, 1024, 2560], P('rep'), parts along dimension 0
- output 2: bfloat16 [4, 1024, 2560], P('rep'), parts along dimension 0
- output 3: bfloat16 [4, 2560, 1024], P('rep'), parts along dimension 0
- output 4: float32 [4, 1024, 2560], P('rep'), parts along dimension 0
- output 5: float32 [4, 1024, 2560], P('rep'), parts along dimension 0
- output 6: float32 [4, 2560, 1024], P('rep'), parts along dimension 0
- output 7: float32 [4, 1024, 2560], P('rep'), parts along dimension 0
- output 8: float32 [4, 1024, 2560], P('rep'), parts along dimension 0
- output 9: float32 [4, 2560, 1024], P('rep'), parts along dimension 0
There are 2 independent parts. A program takes and returns all parts, laid end to end along the dimension named above; an argument that names none is the same for every part.
All inputs are finite; a program needn't handle non-finite values.
Results may differ from a plain program's by a relative error of at most 0.022.
Values are sent between devices in bfloat16 or wider.
A program may use at most 2.5 GiB of HBM per device.

v0:
```python
import jax
import jax.numpy as jnp
from jax import lax
from jax.sharding import PartitionSpec as P

NAMES = ("w_gate", "w_up", "w_down")


def matmul(a, w):
    return jnp.dot(a, w, preferred_element_type=jnp.float32).astype(jnp.bfloat16)


def normed(h):
    wide = h.astype(jnp.float32)
    scale = lax.rsqrt(jnp.mean(wide**2, -1, keepdims=True) + 1e-6)
    return (wide * scale).astype(jnp.bfloat16)


def layer(h, w):
    a = normed(h)
    gate = jnp.dot(a, w["w_gate"], preferred_element_type=jnp.float32)
    up = jnp.dot(a, w["w_up"], preferred_element_type=jnp.float32)
    return h + matmul((jax.nn.silu(gate) * up).astype(jnp.bfloat16), w["w_down"])


def adamw(w, m, v, g):
    m = 0.9 * m + 0.1 * g
    v = 0.95 * v + 0.05 * g * g
    step = m * lax.rsqrt(v + 1e-8) + 0.1 * w
    return (w - 0.02 * step).astype(jnp.bfloat16), m, v


def clipped(gradients, sum_of_squares, count):
    factor = jnp.minimum(1.0, 0.5 * lax.rsqrt(sum_of_squares / count + 1e-30))
    return [g * factor for g in gradients]


def solution(mesh):
    def step(x, dy, *arrays):
        weights, m, v = (arrays[i : i + 3] for i in (0, 3, 6))
        layers = weights[0].shape[0]
        h, kept = x[0], []
        for number in range(layers):
            kept.append(h)
            h = layer(h, {name: w[number] for name, w in zip(NAMES, weights, strict=True)})
        by_h, summed = dy[0], [None] * layers
        for number in reversed(range(layers)):
            _, back = jax.vjp(lambda w, h: layer(h, w), {name: w[number] for name, w in zip(NAMES, weights, strict=True)}, kept[number])
            by_w, by_h = back(by_h)
            summed[number] = [lax.psum(by_w[name], "dp") for name in NAMES]
        gradients = [jnp.stack([summed[number][i] for number in range(layers)]).astype(jnp.float32) for i in range(3)]
        gradients = clipped(gradients, sum(jnp.sum(g * g) for g in gradients), sum(g.size for g in gradients))
        new = [adamw(w.astype(jnp.float32), m, v, g) for w, m, v, g in zip(weights, m, v, gradients, strict=True)]
        return tuple(one[which] for which in range(3) for one in new)

    return jax.shard_map(
        step,
        mesh=mesh,
        in_specs=(P(("rep", "dp"), None, None),) * 2 + (P(None, None, None),) * 9,
        out_specs=(P("rep", None, None),) * 9,
        check_vma=False,
    )
```

profile of v0, /device:TPU:0, one launch (start us, length us, event | category | flops | bytes accessed | tf_op | source)
XLA Modules:
  0.0 992.7 jit_solution(4749268811116766887)
XLA Ops:
  7.2 6.5 copy.20
  16.8 6.7 copy.21
  23.5 16.9 %convolution_convert_fusion.1 = bf16[2048,2560]{1,0:T(8,128)(2,1)} fusion(bf16[2,2560,1024]{2,1,0:T(8,128)(2,1)} %param.15, bf16[1,2048,1024]{2,1,0:T(8,128)(2,1)} %param.12), kind=kOutput, calls=%fused_computation.63 | convolution fusion | flops 10742661120 | bytes 19922944 | tf_op jit(solution)/shard_map/transpose(jvp())/dot_general | solution.py:10
  40.4 14.1 %fusion.62 = f32[2048,2560]{1,0:T(8,128)} fusion(bf16[2,1024,2560]{2,1,0:T(8,128)(2,1)S(1)} %bitcast.77, bf16[1,2048,1024]{2,1,0:T(8,128)(2,1)S(1)} %copy-done.4, f32[2048]{0:T(1024)S(1)} %add_rsqrt_fusion), kind=kOutput, calls=%fused_computation.99 | convolution fusion | flops 10743709696 | bytes 30416896 | tf_op jit(solution)/shard_map/dot_general | solution.py:21
  54.5 26.7 %multiply_convert_fusion.1 = (bf16[2048,2560]{1,0:T(8,128)(2,1)}, f32[2048,2560]{1,0:T(8,128)}) fusion(f32[2048,2560]{1,0:T(8,128)} %fusion.62, bf16[2,1024,2560]{2,1,0:T(8,128)(2,1)} %param.14, bf16[1,2048,1024]{2,1,0:T(8,128)(2,1)} %param.11, f32[2048]{0:T(1024)S(1)} %add_rsqrt_fusion), kind=kOutput, calls=%fused_computation.53 | convolution fusion | flops 10775166976 | bytes 61874176 | tf_op jit(solution)/shard_map/dot_general | solution.py:22
  81.3 17.7 %fusion.40 = (f32[2048]{0:T(1024)S(1)}, bf16[2048,1024]{0,1:T(8,128)(2,1)}) fusion(bf16[2048,2560]{1,0:T(8,128)(2,1)} %get-tuple-element.24, bf16[2,2560,1024]{2,1,0:T(8,128)(2,1)} %param.15, bf16[1,2048,1024]{1,2,0:T(8,128)(2,1)S(1)} %copy-done.2), kind=kOutput, calls=%fused_computation.76 | convolution fusion | flops 10747901952 | bytes 24125440 | tf_op jit(solution)/shard_map/dot_general | solution.py:10
  98.9 18.5 %fusion.49 = f32[2048,2560]{1,0:T(8,128)} fusion(bf16[2,1024,2560]{2,1,0:T(8,128)(2,1)} %param.14, bf16[2048,1024]{0,1:T(8,128)(2,1)} %get-tuple-element.27, f32[2048]{0:T(1024)S(1)} %fusion.98), kind=kOutput, calls=%fused_computation.86 | convolution fusion | flops 10743709696 | bytes 30416896 | tf_op jit(solution)/shard_map/jvp()/dot_general | solution.py:22
  117.4 32.4 %fusion.20 = (bf16[2048,2560]{1,0:T(8,128)(2,1)}, f32[2048,2560]{1,0:T(8,128)}) fusion(f32[2048,2560]{1,0:T(8,128)} %fusion.49, bf16[2048,2560]{1,0:T(8,128)(2,1)} %convolution_convert_fusion.1, bf16[2,1024,2560]{2,1,0:T(8,128)(2,1)} %param.13, bf16[2048,1024]{0,1:T(8,128)(2,1)} %get-tuple-element.27, f32[2048]{0:T(1024)S(1)} %fusion.98), kind=kOutput, calls=%fused_computation.41 | convolution fusion | flops 10806624256 | bytes 72359936 | tf_op jit(solution)/shard_map/jvp()/dot_general | solution.py:21
  149.8 19.9 %fusion.33 = bf16[2048,1024]{0,1:T(8,128)(2,1)} fusion(bf16[2048,2560]{1,0:T(8,128)(2,1)} %convolution_convert_fusion.1, bf16[2,1024,2560]{2,1,0:T(8,128)(2,1)} %param.14, f32[2048,2560]{1,0:T(8,128)} %get-tuple-element.29), kind=kOutput, calls=%fused_computation.61 | convolution fusion | flops 10768875520 | bytes 40894464 | tf_op jit(solution)/shard_map/transpose(jvp())/dot_general | solution.py:22
  169.7 20.0 %fusion.71 = bf16[1,1024,2560]{2,1,0:T(8,128)(2,1)} fusion(bf16[2048,2560]{1,0:T(8,128)(2,1)} %convolution_convert_fusion.1, bf16[2048,1024]{0,1:T(8,128)(2,1)} %get-tuple-element.27, f32[2048]{0:T(1024)S(1)} %fusion.98, f32[2048,2560]{1,0:T(8,128)} %get-tuple-element.29), kind=kOutput, calls=%fused_computation.106 | convolution fusion | flops 10777788416 | bytes 40902656 | tf_op jit(solution)/shard_map/transpose(jvp())/dot_general | solution.py:22
  189.7 22.1 %fusion.72 = bf16[1,2560,1024]{2,1,0:T(8,128)(2,1)} fusion(f32[2048,2560]{1,0:T(8,128)} %fusion.49, bf16[1,2048,1024]{2,1,0:T(8,128)(2,1)} %param.12, f32[2048,2560]{1,0:T(8,128)} %get-tuple-element.29), kind=kOutput, calls=%fused_computation.107 | convolution fusion | flops 10771496960 | bytes 51380224 | tf_op jit(solution)/shard_map/transpose(jvp())/dot_general | solution.py:10
  211.8 16.6 %fusion.73 = bf16[1,1024,2560]{2,1,0:T(8,128)(2,1)} fusion(bf16[2048,2560]{1,0:T(8,128)(2,1)} %get-tuple-element.28, bf16[2048,1024]{0,1:T(8,128)(2,1)} %get-tuple-element.27, f32[2048]{0:T(1024)S(1)} %fusion.98), kind=kOutput, calls=%fused_computation.108 | convolution fusion | flops 10743709696 | bytes 19931136 | tf_op jit(solution)/shard_map/transpose(jvp())/dot_general | solution.py:21
  228.4 16.8 %fusion.42 = (f32[2048]{0:T(1024)S(1)}, bf16[2048,1024]{0,1:T(8,128)(2,1)S(1)}) fusion(bf16[2048,1024]{0,1:T(8,128)(2,1)S(1)} %copy-done.3, bf16[2048,1024]{0,1:T(8,128)(2,1)} %fusion.33, bf16[2048,2560]{1,0:T(8,128)(2,1)} %get-tuple-element.28, bf16[2,1024,2560]{2,1,0:T(8,128)(2,1)} %param.13), kind=kOutput, calls=%fused_computation.78 | convolution fusion | flops 10747901952 | bytes 28319744 | tf_op jit(solution)/shard_map/transpose(jvp())/dot_general | solution.py:21
  245.3 3.2 fusion.82
  248.4 15.8 %convolution_convert_fusion = bf16[2048,2560]{1,0:T(8,128)(2,1)} fusion(bf16[2048,1024]{0,1:T(8,128)(2,1)S(1)} %fusion.82, bf16[2,2560,1024]{2,1,0:T(8,128)(2,1)} %param.15), kind=kOutput, calls=%fused_computation.62 | convolution fusion | flops 10742661120 | bytes 19922944 | tf_op jit(solution)/shard_map/transpose(jvp())/dot_general | solution.py:10
  264.3 15.6 %fusion.74 = bf16[1,2560,1024]{2,1,0:T(8,128)(2,1)} fusion(bf16[2048,2560]{1,0:T(8,128)(2,1)} %get-tuple-element.24, bf16[2048,1024]{0,1:T(8,128)(2,1)S(1)} %fusion.82), kind=kOutput, calls=%fused_computation.109 | convolution fusion | flops 10740039680 | bytes 19922944 | tf_op jit(solution)/shard_map/transpose(jvp())/dot_general | solution.py:10
  279.9 20.1 %fusion.67 = bf16[1,1024,2560]{2,1,0:T(8,128)(2,1)} fusion(bf16[2048,2560]{1,0:T(8,128)(2,1)} %convolution_convert_fusion, bf16[1,2048,1024]{1,2,0:T(8,128)(2,1)} %copy.20, f32[2048]{0:T(1024)S(1)} %copy-done.8, f32[2048,2560]{1,0:T(8,128)} %fusion.62), kind=kOutput, calls=%fused_computation.104 | convolution fusion | flops 10777788416 | bytes 40902656 | tf_op jit(solution)/shard_map/transpose(jvp())/dot_general | solution.py:22
  300.0 24.9 %fusion.68 = bf16[1,1024,2560]{2,1,0:T(8,128)(2,1)} fusion(f32[2048,2560]{1,0:T(8,128)} %fusion.62, f32[2048,2560]{1,0:T(8,128)} %get-tuple-element.25, bf16[2048,2560]{1,0:T(8,128)(2,1)} %convolution_convert_fusion, bf16[1,2048,1024]{1,2,0:T(8,128)(2,1)} %copy.20, f32[2048]{0:T(1024)S(1)} %copy-done.8), kind=kOutput, calls=%fused_computation.105 | convolution fusion | flops 10804002816 | bytes 61874176 | tf_op jit(solution)/shard_map/transpose(jvp())/dot_general | solution.py:21
  324.9 521.6 %all-reduce.3.cloned.1.call-done = (bf16[1,1024,2560]{2,1,0:T(8,128)(2,1)}, bf16[1,1024,2560]{2,1,0:T(8,128)(2,1)}, bf16[1,1024,2560]{2,1,0:T(8,128)(2,1)}, bf16...) async-done(((bf16[1,1024,2560]{2,1,0:T(8,128)(2,1)}, bf16[1,1024,2560]{2,1,0:T(8,128)(2,1)}, ...) | async-done | bytes 31457296 | tf_op jit(solution)/shard_map/psum | solution.py:50
  846.4 9.4 fusion.10
  855.9 6.0 fusion.11
  863.2 8.5 fusion.12
  872.4 40.2 %fusion.18 = (bf16[2,2560,1024]{2,1,0:T(8,128)(2,1)}, f32[2,2560,1024]{2,1,0:T(8,128)}, f32[2,2560,1024]{2,1,0:T(8,128)}) fusion(bf16[2,2560,1024]{2,1,0:T(8,128)(2,1)} %param.15, f32[]{:T(128)S(6)} %min_shard_map.3, bf16[1,2560,1024]{2,1,0:T(8,128)(2,1)} %get-tuple-element.13, bf16[1,2560,1024]{2,1,0:T(8,128)(2,1)} %get-tuple-element.14, ...), kind=kLoop, calls=%fused_computation.39 | loop fusion | flops 104857600 | bytes 115343360 | tf_op jit(solution)/shard_map/convert_element_type | solution.py:30
  912.6 72.8 %fusion.8 = (bf16[2,1024,2560]{2,1,0:T(8,128)(2,1)}, f32[2,1024,2560]{2,1,0:T(8,128)}, f32[2,1024,2560]{2,1,0:T(8,128)}, bf16[2,1024,2560]{2,1,0:T(8,128)(2,1)},...) fusion(bf16[2,1024,2560]{2,1,0:T(8,128)(2,1)} %param.13, f32[]{:T(128)S(6)} %min_shard_map.3, ...), kind=kLoop, calls=%fused_computation.29 | loop fusion | flops 209715200 | bytes 230686720 | tf_op jit(solution)/shard_map/convert_element_type | solution.py:30
  (36 shorter events, 3.2 us)
Async XLA Ops:
  7.2 839.3 %all-reduce.3.cloned.1.call-start = ((), (), s32[]{:S(2)}) async-start(), calls=%async_computation | async-start | bytes 62914560 | tf_op jit(solution)/shard_map/psum | solution.py:50
  16.8 37.7 %copy-start.7 = (f32[2048]{0:T(1024)}, f32[2048]{0:T(1024)S(1)}, u32[]{:S(2)}) copy-start(f32[2048]{0:T(1024)S(1)} %add_rsqrt_fusion) | copy-start | bytes 24580
  16.8 23.6 %slice-start.2 = ((s8[10485760]{0:T(1024)(128)(4,1)}), s8[2097152]{0:T(1024)(128)(4,1)S(1)}, s32[]{:S(2)}) async-start(s8[10485760]{0:T(1024)(128)(4,1)} %bitcast.76), calls=%async_computation.3 | async-start | bytes 4194304
  23.5 16.9 %slice-start.3 = ((s8[10485760]{0:T(1024)(128)(4,1)}), s8[4194304]{0:T(1024)(128)(4,1)S(1)}, s32[]{:S(2)}) async-start(s8[10485760]{0:T(1024)(128)(4,1)} %bitcast.76), calls=%async_computation.4 | async-start | bytes 8388608
  23.5 16.9 %slice-start.4 = ((s8[10485760]{0:T(1024)(128)(4,1)}), s8[4194304]{0:T(1024)(128)(4,1)S(1)}, s32[]{:S(2)}) async-start(s8[10485760]{0:T(1024)(128)(4,1)} %bitcast.76), calls=%async_computation.5 | async-start | bytes 8388608
  23.5 16.9 %copy-start.4 = (bf16[1,2048,1024]{2,1,0:T(8,128)(2,1)S(1)}, bf16[1,2048,1024]{2,1,0:T(8,128)(2,1)}, u32[]{:S(2)}) copy-start(bf16[1,2048,1024]{2,1,0:T(8,128)(2,1)} %param.11) | copy-start | bytes 12582916
  54.5 26.7 %copy-start.2 = (bf16[1,2048,1024]{1,2,0:T(8,128)(2,1)S(1)}, bf16[1,2048,1024]{1,2,0:T(8,128)(2,1)}, u32[]{:S(2)}) copy-start(bf16[1,2048,1024]{1,2,0:T(8,128)(2,1)} %copy.20) | copy-start | bytes 12582916
  98.9 18.5 %copy-start.5 = (f32[2048]{0:T(1024)}, f32[2048]{0:T(1024)S(1)}, u32[]{:S(2)}) copy-start(f32[2048]{0:T(1024)S(1)} %get-tuple-element.26) | copy-start | bytes 24580
  211.8 16.6 %copy-start.3 = (bf16[2048,1024]{0,1:T(8,128)(2,1)S(1)}, bf16[2048,1024]{0,1:T(8,128)(2,1)}, u32[]{:S(2)}) copy-start(bf16[2048,1024]{0,1:T(8,128)(2,1)} %get-tuple-element.27) | copy-start | bytes 12582916
  228.4 16.8 %copy-start.6 = (f32[2048]{0:T(1024)S(1)}, f32[2048]{0:T(1024)}, u32[]{:S(2)}) copy-start(f32[2048]{0:T(1024)} %copy-done.5) | copy-start | bytes 24580
  228.4 16.9 %copy-start.1 = (bf16[1,2048,1024]{1,2,0:T(8,128)(2,1)S(1)}, bf16[1,2048,1024]{1,2,0:T(8,128)(2,1)}, u32[]{:S(2)}) copy-start(bf16[1,2048,1024]{1,2,0:T(8,128)(2,1)} %copy.21) | copy-start | bytes 12582916
  264.3 15.6 %copy-start.8 = (f32[2048]{0:T(1024)S(1)}, f32[2048]{0:T(1024)}, u32[]{:S(2)}) copy-start(f32[2048]{0:T(1024)} %copy-done.7) | copy-start | bytes 24580
  846.4 9.5 slice-start
  846.4 9.5 copy-start
  846.4 9.5 slice-start.1
Sparse Core Ops, SparseCore 0:
  325.0 521.3 all-reduce.2
where the time goes:
time: 1000 us; the launch traced here: 993 us
  waiting for transfers between devices  522 us (52%)
  matrix products  298 us (30%)
  other arithmetic  143 us (14%)
  between operations  16.6 us (2%)
  local copies, waits for them, and re-layouts  13.2 us (1%)
    psum x1, waiting for transfers between devices, step(): summed[number] = [lax.psum(by_w[name], 'dp') for name in NAMES]  522 us
    convert_element_type x2, other arithmetic, adamw(): return ((w - 0.02 * step).astype(jnp.bfloat16), m, v)  113 us
    dot_general x5, matrix products, layer(): up = jnp.dot(a, w['w_up'], preferred_element_type=jnp.float32)  105 us
    dot_general x5, matrix products, layer(): gate = jnp.dot(a, w['w_gate'], preferred_element_type=jnp.float32)  105 us
    dot_general x5, matrix products, matmul(): jnp.dot(a, w, preferred_element_type=jnp.float32).astype(jnp.bfloat16)  88.1 us
    reduce_sum x3, other arithmetic, step(): jnp.sum(g * g)  24 us
  transfers between devices with their start and end apart: 1, of which 1 were waited for; matrix products, arithmetic and copies ran while one was open for 0% of the time, Pallas kernels for 0%

commit v1 on v0

v1 whole, which is shorter than its diff:
```python
import jax
import jax.numpy as jnp
from jax import lax
from jax.experimental import pallas as pl
from jax.experimental.pallas import tpu as pltpu
from jax.sharding import PartitionSpec as P

F32, BF16 = jnp.float32, jnp.bfloat16
J = 256
ROWS = 512
LAG = 3
FAR = 2 * LAG + 2
VMEM_LIMIT = 67043328
MESH = pl.DeviceIdType.MESH


def dot(a, b):
    return jnp.dot(a, b, preferred_element_type=F32)


def dot_nt(a, b):
    return lax.dot_general(a, b, (((1,), (1,)), ((), ())), preferred_element_type=F32)


def norm_scale(wide):
    return lax.rsqrt(jnp.mean(wide**2, -1, keepdims=True) + 1e-6)


def gradients(x_hbm, dy_hbm, wg_hbm, wu_hbm, wd_hbm, g_hbm, ss_ref, h, a, at, dh, dht, acc0, acc1, act, dg, du, wg, wu, wd,
              grad, near, chip, far, total, ssv, ssr, w_sem, x_sem, s1_send, s1_recv, s2_send, s2_recv, s3_send, s3_recv, put_sem, ss_sem):
    tokens, d = h.shape
    blocks = tokens // ROWS
    n = wg_hbm.shape[2] // J
    steps = 2 * n
    half = d // 2
    me = lax.axis_index("dp")
    core = lax.rem(me, 2)
    partner = me + 1 - 2 * core
    across = lax.rem(me + 2, 4)

    def rows(r):
        return pl.ds(pl.multiple_of(r * ROWS, ROWS), ROWS)

    def weight_copies(f):
        slot, layer, j = lax.rem(f, 2), lax.rem(f // n, 2), lax.rem(f, n)
        cols = pl.ds(pl.multiple_of(j * J, J), J)
        return [
            pltpu.make_async_copy(wg_hbm.at[layer, :, cols], wg.at[slot], w_sem.at[0, slot]),
            pltpu.make_async_copy(wu_hbm.at[layer, :, cols], wu.at[slot], w_sem.at[1, slot]),
            pltpu.make_async_copy(wd_hbm.at[layer, cols, :], wd.at[slot], w_sem.at[2, slot]),
        ]

    def next_weights(f):
        for copy in weight_copies(f):
            copy.wait()

        @pl.when(f + 1 < 3 * n)
        def _():
            for copy in weight_copies(f + 1):
                copy.start()

        return lax.rem(f, 2)

    for copy in weight_copies(0):
        copy.start()
    get_x = pltpu.make_async_copy(x_hbm, h, x_sem.at[0])
    get_x.start()
    get_dy = pltpu.make_async_copy(dy_hbm, dh, x_sem.at[1])
    get_dy.start()
    barrier = pltpu.get_barrier_semaphore()
    for other in (partner, across):
        pl.semaphore_signal(barrier, inc=1, device_id={"dp": other}, device_id_type=MESH)
    pl.semaphore_wait(barrier, 2)
    ssv[...] = jnp.zeros_like(ssv)

    get_x.wait()

    def norm_block(r, _):
        wide = h[rows(r), :].astype(F32)
        a[rows(r), :] = (wide * norm_scale(wide)).astype(BF16)
        acc0[rows(r), :] = jnp.zeros((ROWS, d), F32)
        return 0

    lax.fori_loop(0, blocks, norm_block, 0)

    def forward(j, _):
        slot = next_weights(j)
        for r in range(blocks):
            here = pl.ds(r * ROWS, ROWS)
            block = a[here, :]
            gate = dot(block, wg[slot])
            up = dot(block, wu[slot])
            acc0[here, :] += dot((gate * jax.nn.sigmoid(gate) * up).astype(BF16), wd[slot])
        return 0

    lax.fori_loop(0, n, forward, 0)
    get_dy.wait()

    def turn(r, _):
        at[:, rows(r)] = a[rows(r), :].T
        dht[:, rows(r)] = dh[rows(r), :].T
        return 0

    def to_layer_1(r, _):
        new = h[rows(r), :] + acc0[rows(r), :].astype(BF16)
        h[rows(r), :] = new
        wide = new.astype(F32)
        a[rows(r), :] = (wide * norm_scale(wide)).astype(BF16)
        acc0[rows(r), :] = jnp.zeros((ROWS, d), F32)
        acc1[rows(r), :] = jnp.zeros((ROWS, d), F32)
        return turn(r, 0)

    lax.fori_loop(0, blocks, to_layer_1, 0)

    def to_layer_0(r, _):
        by_a = (acc0[rows(r), :].astype(BF16).astype(F32) + acc1[rows(r), :].astype(BF16).astype(F32)).astype(BF16).astype(F32)
        wide = h[rows(r), :].astype(F32)
        mean = jnp.mean(wide**2, -1, keepdims=True) + 1e-6
        scale = lax.rsqrt(mean)
        by_scale = jnp.sum(by_a * wide, -1, keepdims=True)
        by_wide = by_a * scale - wide * (by_scale * scale / mean * (1.0 / d))
        dh[rows(r), :] = (dh[rows(r), :].astype(F32) + by_wide.astype(BF16).astype(F32)).astype(BF16)
        return 0

    def again(r, _):
        wide = h[rows(r), :].astype(F32)
        a[rows(r), :] = (wide * norm_scale(wide)).astype(BF16)
        return turn(r, 0)

    def s1(t):
        slot = lax.rem(t, 2)
        return pltpu.make_async_remote_copy(
            src_ref=grad.at[:, pl.ds(pl.multiple_of((1 - core) * half, half), half), :], dst_ref=near.at[slot],
            send_sem=s1_send, recv_sem=s1_recv.at[slot], device_id={"dp": partner}, device_id_type=MESH)

    def s2(t):
        return pltpu.make_async_remote_copy(
            src_ref=chip.at[lax.rem(t, LAG + 1)], dst_ref=far.at[lax.rem(t, FAR)], send_sem=s2_send.at[lax.rem(t, LAG + 1)],
            recv_sem=s2_recv.at[lax.rem(t, FAR)], device_id={"dp": across}, device_id_type=MESH)

    def place(t, which):
        return g_hbm.at[t, :, pl.ds(pl.multiple_of(which * half, half), half), :]

    def s3(t):
        return pltpu.make_async_remote_copy(
            src_ref=total.at[lax.rem(t, 2)], dst_ref=place(t, core), send_sem=s3_send.at[lax.rem(t, 2)], recv_sem=s3_recv.at[t],
            device_id={"dp": partner}, device_id_type=MESH)

    def put(t):
        return pltpu.make_async_copy(total.at[lax.rem(t, 2)], place(t, core), put_sem.at[lax.rem(t, 2)])

    def step(t, _):
        @pl.when(t < steps)
        def _():
            @pl.when(t == n)
            def _():
                lax.fori_loop(0, blocks, to_layer_0, 0)
                again_x = pltpu.make_async_copy(x_hbm, h, x_sem.at[0])
                again_x.start()
                again_x.wait()
                lax.fori_loop(0, blocks, again, 0)

            slot = next_weights(n + t)

            def block(r, _):
                here = rows(r)
                gate = dot(a[here, :], wg[slot])
                up = dot(a[here, :], wu[slot])
                by_act = dot_nt(dh[here, :], wd[slot]).astype(BF16).astype(F32)
                s = jax.nn.sigmoid(gate)
                silu = gate * s
                act[here, :] = (silu * up).astype(BF16)
                du[here, :] = (by_act * silu).astype(BF16)
                dg[here, :] = (by_act * up * (s + silu * (1.0 - s))).astype(BF16)
                return 0

            lax.fori_loop(0, blocks, block, 0, unroll=2)

            def rest(r, _):
                here = rows(r)
                grad[0, here, :] = dot(at[here, :], dg[...]).astype(BF16)
                grad[1, here, :] = dot(at[here, :], du[...]).astype(BF16)
                grad[2, here, :] = dot(dht[here, :], act[...]).astype(BF16)
                return 0

            lax.fori_loop(0, d // ROWS, rest, 0)
            s1(t).start()

            @pl.when(t < n)
            def _():
                def back(r, _):
                    here = rows(r)
                    acc0[here, :] += dot_nt(dg[here, :], wg[slot])
                    acc1[here, :] += dot_nt(du[here, :], wu[slot])
                    return 0

                lax.fori_loop(0, blocks, back, 0)

            s1(t).wait()
            own = pl.ds(pl.multiple_of(core * half, half), half)
            for k in range(3):
                chip[lax.rem(t, LAG + 1), k] = (grad[k, own, :].astype(F32) + near[lax.rem(t, 2), k].astype(F32)).astype(BF16)
            s2(t).start()

        @pl.when(t >= LAG)
        def _():
            u = t - LAG

            @pl.when(u >= 2)
            def _():
                s3(u - 2).wait_send()
                put(u - 2).wait()

            s2(u).wait()
            for k in range(3):
                new = (chip[lax.rem(u, LAG + 1), k].astype(F32) + far[lax.rem(u, FAR), k].astype(F32)).astype(BF16)
                total[lax.rem(u, 2), k] = new
                wide = new.astype(F32)
                ssv[...] += jnp.sum((wide * wide).reshape(half // 8, 8, J), 0)
            s3(u).start()
            put(u).start()

        return 0

    lax.fori_loop(0, steps + LAG, step, 0)
    share = pltpu.make_async_remote_copy(
        src_ref=ssv, dst_ref=ssr, send_sem=ss_sem.at[0], recv_sem=ss_sem.at[1], device_id={"dp": partner}, device_id_type=MESH)
    share.start()
    for u in (steps - 2, steps - 1):
        s3(u).wait_send()
        put(u).wait()

    def arrived(t, _):
        s3(t).wait_recv()
        return 0

    lax.fori_loop(0, steps, arrived, 0)
    share.wait()
    ss_ref[...] = ssv[...] + ssr[...]


def call_gradients(x, dy, wg, wu, wd):
    tokens, d = x.shape
    n = wg.shape[2] // J
    half = d // 2
    hbm = pl.BlockSpec(memory_space=pl.ANY)
    dma = pltpu.SemaphoreType.DMA
    return pl.pallas_call(
        gradients,
        name="gradients",
        out_shape=(jax.ShapeDtypeStruct((2 * n, 3, d, J), BF16), jax.ShapeDtypeStruct((8, J), F32)),
        in_specs=[hbm] * 5,
        out_specs=(hbm, pl.BlockSpec(memory_space=pltpu.VMEM)),
        scratch_shapes=[
            pltpu.VMEM((tokens, d), BF16), pltpu.VMEM((tokens, d), BF16), pltpu.VMEM((d, tokens), BF16),
            pltpu.VMEM((tokens, d), BF16), pltpu.VMEM((d, tokens), BF16),
            pltpu.VMEM((tokens, d), F32), pltpu.VMEM((tokens, d), F32),
            pltpu.VMEM((tokens, J), BF16), pltpu.VMEM((tokens, J), BF16), pltpu.VMEM((tokens, J), BF16),
            pltpu.VMEM((2, d, J), BF16), pltpu.VMEM((2, d, J), BF16), pltpu.VMEM((2, J, d), BF16),
            pltpu.VMEM((3, d, J), BF16), pltpu.VMEM((2, 3, half, J), BF16), pltpu.VMEM((LAG + 1, 3, half, J), BF16),
            pltpu.VMEM((FAR, 3, half, J), BF16), pltpu.VMEM((2, 3, half, J), BF16),
            pltpu.VMEM((8, J), F32), pltpu.VMEM((8, J), F32),
            dma((3, 2)), dma((2,)), dma, dma((2,)), dma((LAG + 1,)), dma((FAR,)), dma((2,)), dma((2 * n,)), dma((2,)), dma((2,)),
        ],
        compiler_params=pltpu.CompilerParams(collective_id=0, has_side_effects=True, vmem_limit_bytes=VMEM_LIMIT),
    )(x, dy, wg, wu, wd)


def adamw(count, ss, g, wg, wu, wd, mg, mu, md, vg, vu, vd, *outs):
    squares = jnp.sum(jnp.sum(ss[...], 0, keepdims=True), 1, keepdims=True)
    factor = jnp.minimum(1.0, 0.5 * lax.rsqrt(squares / count + 1e-30))
    for k, (w, m, v) in enumerate(((wg, mg, vg), (wu, mu, vu), (wd, md, vd))):
        mine = g[0, k].astype(F32)
        mine = (mine.T if k == 2 else mine) * factor
        new_m = 0.9 * m[0] + 0.1 * mine
        new_v = 0.95 * v[0] + 0.05 * mine * mine
        w_out, m_out, v_out = outs[k], outs[3 + k], outs[6 + k]
        old = w[0].astype(F32)
        w_out[0] = (old - 0.02 * (new_m * lax.rsqrt(new_v + 1e-8) + 0.1 * old)).astype(BF16)
        m_out[0] = new_m
        v_out[0] = new_v


def call_adamw(ss, g, weights, m, v):
    layers, d, ff = weights[0].shape
    n = ff // J
    wide = pl.BlockSpec((1, d, J), lambda l, j: (l, 0, j))
    tall = pl.BlockSpec((1, J, d), lambda l, j: (l, j, 0))
    three = [wide, wide, tall]
    count = float(3 * layers * d * ff)
    return pl.pallas_call(
        lambda *refs: adamw(count, *refs),
        name="adamw",
        grid=(layers, n),
        out_shape=[jax.ShapeDtypeStruct(w.shape, t) for t in (BF16, F32, F32) for w in weights],
        in_specs=[pl.BlockSpec((8, J), lambda l, j: (0, 0)), pl.BlockSpec((1, 3, d, J), lambda l, j: ((layers - 1 - l) * n + j, 0, 0, 0))] + three * 3,
        out_specs=three * 3,
        compiler_params=pltpu.CompilerParams(vmem_limit_bytes=VMEM_LIMIT),
    )(ss, g, *weights, *m, *v)


def solution(mesh):
    def step(x, dy, *arrays):
        weights, m, v = (arrays[i : i + 3] for i in (0, 3, 6))
        g, ss = call_gradients(x[0], dy[0], *weights)
        return tuple(call_adamw(ss, g, weights, m, v))

    return jax.shard_map(
        step,
        mesh=mesh,
        in_specs=(P(("rep", "dp"), None, None),) * 2 + (P(None, None, None),) * 9,
        out_specs=(P("rep", None, None),) * 9,
        check_vma=False,
    )
```

time: 1000 us -> 513 us (0.51)
  waiting for transfers between devices: 522 us -> 0 us
  Pallas kernels: 0 us -> 512 us
  matrix products: 298 us -> 0 us
  other arithmetic: 143 us -> 0 us
  between operations: 16.6 us -> 0.81 us
  local copies, waits for them, and re-layouts: 13.2 us -> 0 us
    psum x1 -> x0, waiting for transfers between devices: 522 us -> none  [step(): summed[number] = [lax.psum(by_w[name], 'dp') for name in NAMES]]
    pallas_call x0 -> x2, Pallas kernels: none -> 512 us  [the longest x1 399 us: call_gradients(): pl.pallas_call(gradients, name='gradients', out_shape=(jax.ShapeDtypeStru...]
    dot_general x15 -> x0, matrix products: 298 us -> none  [the longest x5 105 us: layer(): up = jnp.dot(a, w['w_up'], preferred_element_type=jnp.float32)]
    convert_element_type x2 -> x0, other arithmetic: 113 us -> none  [adamw(): return ((w - 0.02 * step).astype(jnp.bfloat16), m, v)]
    reduce_sum x4 -> x0, other arithmetic: 27 us -> none  [the longest x3 24 us: step(): jnp.sum(g * g)]
    unnamed x30 -> x0, local copies, waits for them, and re-layouts: 13.2 us -> none
  transfers between devices with their start and end apart: 1 -> 0, of which waited for: 1 -> 0; matrix products, arithmetic and copies ran while one was open for 0% -> 0% of each run, Pallas kernels for 0% -> 0%
where the time goes in v1:
time: 513 us; the launch traced here: 512 us
  Pallas kernels  512 us (100%)
    pallas_call x1, Pallas kernels, call_gradients(): pl.pallas_call(gradients, name='gradients', out_shape=(jax.ShapeDtypeStru...  399 us
    pallas_call x1, Pallas kernels, call_adamw(): pl.pallas_call(lambda *refs: adamw(count, *refs), name='adamw', grid=(lay...  112 us

profile of v1, /device:TPU:0, one launch (start us, length us, event | category | flops | bytes accessed | tf_op | source)
XLA Modules:
  0.0 512.5 jit_solution(12402291748272249645)
XLA Ops:
  0.6 399.5 %gradients.1 = (bf16[20,3,1024,256]{3,2,1,0:T(8,128)(2,1)}, f32[8,256]{1,0:T(8,128)}) custom-call(bf16[2048,1024]{1,0:T(8,128)(2,1)} %bitcast.2, bf16[2048,1024]{1,0:T(8,128)(2,1)} %bitcast.3, bf16[2,1024,2560]{2,1,0:T(8,128)(2,1)} %refs_2_.1, bf16[2,1024,2560]{2,1,0:T(8,128)(2,1)} %refs_3_.1, bf16[2,2560,1024]{2,1,0:T(8,128)(2,1)} %refs_4_.1), custom_call_target="tpu_custom_call" | custom-call | tf_op jit(solution)/shard_map/gradients/pallas_call | solution.py:248
  400.1 112.2 %adamw.1 = (bf16[2,1024,2560]{2,1,0:T(8,128)(2,1)}, bf16[2,1024,2560]{2,1,0:T(8,128)(2,1)}, bf16[2,2560,1024]{2,1,0:T(8,128)(2,1)}, f32[2,1024,2560]{2,1,0:T(8,1...) custom-call(f32[8,256]{1,0:T(8,128)} %get-tuple-element.11.refs_0_, ...), custom_call_target="tpu_custom_call" | custom-call | tf_op jit(solution)/shard_map/adamw/pallas_call | solution.py:291

commit v2 on v1

v2 whole, which is shorter than its diff:
```python
import jax
import jax.numpy as jnp
from jax import lax
from jax.experimental import pallas as pl
from jax.experimental.pallas import tpu as pltpu
from jax.sharding import PartitionSpec as P

F32, BF16 = jnp.float32, jnp.bfloat16
J = 256
ROWS = 512
VMEM_LIMIT = 67043328
MESH = pl.DeviceIdType.MESH


def dot(a, b):
    return jnp.dot(a, b, preferred_element_type=F32)


def dot_nt(a, b):
    return lax.dot_general(a, b, (((1,), (1,)), ((), ())), preferred_element_type=F32)


def norm_scale(wide):
    return lax.rsqrt(jnp.mean(wide**2, -1, keepdims=True) + 1e-6)


def gradients(x_hbm, dy_hbm, wg_hbm, wu_hbm, wd_hbm, g_hbm, ss_ref, h_hbm, far_h, far_dy, own_hbm, h, a, at, dh, dht, acc, act, dgu, wgu, wd,
              grad, mine, near, chip, far, total, ssv, ssr, w_sem, x_sem, own_sem, far_send, far_recv, s1_send, s1_recv, s2_send, s2_recv,
              s3_send, s3_recv, put_sem, ss_sem):
    tokens, d = h.shape
    blocks = tokens // ROWS
    n = wg_hbm.shape[2] // J
    half = d // 2
    me = lax.axis_index("dp")
    core = lax.rem(me, 2)
    partner = me + 1 - 2 * core
    across = lax.rem(me + 2, 4)

    def rows(r):
        return pl.ds(pl.multiple_of(r * ROWS, ROWS), ROWS)

    def half_of(which):
        return pl.ds(pl.multiple_of(which * half, half), half)

    def weight_copies(f):
        slot, layer, j = lax.rem(f, 2), lax.rem(f // n, 2), lax.rem(f, n)
        cols = pl.ds(pl.multiple_of(j * J, J), J)
        return [
            pltpu.make_async_copy(wg_hbm.at[layer, :, cols], wgu.at[slot, :, pl.ds(0, J)], w_sem.at[0, slot]),
            pltpu.make_async_copy(wu_hbm.at[layer, :, cols], wgu.at[slot, :, pl.ds(J, J)], w_sem.at[1, slot]),
            pltpu.make_async_copy(wd_hbm.at[layer, cols, :], wd.at[slot], w_sem.at[2, slot]),
        ]

    def next_weights(f):
        for copy in weight_copies(f):
            copy.wait()

        @pl.when(f + 1 < 4 * n)
        def _():
            for copy in weight_copies(f + 1):
                copy.start()

        return lax.rem(f, 2)

    def to_across(src, dst, k):
        return pltpu.make_async_remote_copy(
            src_ref=src, dst_ref=dst, send_sem=far_send.at[k], recv_sem=far_recv.at[k], device_id={"dp": across}, device_id_type=MESH)

    for copy in weight_copies(0):
        copy.start()
    get_x = pltpu.make_async_copy(x_hbm, h, x_sem.at[0])
    get_x.start()
    get_dy = pltpu.make_async_copy(dy_hbm, dh, x_sem.at[1])
    get_dy.start()
    barrier = pltpu.get_barrier_semaphore()
    for other in (partner, across):
        pl.semaphore_signal(barrier, inc=1, device_id={"dp": other}, device_id_type=MESH)
    pl.semaphore_wait(barrier, 2)
    send_dy = to_across(dy_hbm, far_dy, 0)
    send_dy.start()
    ssv[...] = jnp.zeros_like(ssv)
    get_x.wait()

    def first_norm(r, _):
        wide = h[rows(r), :].astype(F32)
        a[rows(r), :] = (wide * norm_scale(wide)).astype(BF16)
        acc[rows(r), :] = jnp.zeros((ROWS, d), F32)
        return 0

    lax.fori_loop(0, blocks, first_norm, 0)

    def forward(j, _):
        slot = next_weights(j)
        for r in range(blocks):
            here = pl.ds(r * ROWS, ROWS)
            both = dot(a[here, :], wgu[slot])
            gate, up = both[:, :J], both[:, J:]
            acc[here, :] += dot((gate * jax.nn.sigmoid(gate) * up).astype(BF16), wd[slot])
        return 0

    lax.fori_loop(0, n, forward, 0)

    def end_layer_0(r, _):
        h[rows(r), :] = h[rows(r), :] + acc[rows(r), :].astype(BF16)
        acc[rows(r), :] = jnp.zeros((ROWS, d), F32)
        return 0

    lax.fori_loop(0, blocks, end_layer_0, 0)
    keep_h = pltpu.make_async_copy(h, h_hbm, x_sem.at[0])
    keep_h.start()
    get_dy.wait()
    keep_h.wait()
    send_h = to_across(h_hbm, far_h, 1)
    send_h.start()

    def to_layer_0(r, _):
        by_a = acc[rows(r), :].astype(BF16).astype(F32)
        wide = h[rows(r), :].astype(F32)
        mean = jnp.mean(wide**2, -1, keepdims=True) + 1e-6
        scale = lax.rsqrt(mean)
        by_scale = jnp.sum(by_a * wide, -1, keepdims=True)
        by_wide = by_a * scale - wide * (by_scale * scale / mean * (1.0 / d))
        dh[rows(r), :] = (dh[rows(r), :].astype(F32) + by_wide.astype(BF16).astype(F32)).astype(BF16)
        return 0

    def begin(r, _):
        wide = h[rows(r), :].astype(F32)
        a[rows(r), :] = (wide * norm_scale(wide)).astype(BF16)
        at[:, rows(r)] = a[rows(r), :].T
        dht[:, rows(r)] = dh[rows(r), :].T
        return 0

    def s1(u):
        slot = lax.rem(u, 2)
        return pltpu.make_async_remote_copy(
            src_ref=grad.at[:, half_of(1 - core), :], dst_ref=near.at[slot],
            send_sem=s1_send, recv_sem=s1_recv.at[slot], device_id={"dp": partner}, device_id_type=MESH)

    def s2(j):
        return pltpu.make_async_remote_copy(
            src_ref=chip.at[j], dst_ref=far.at[j], send_sem=s2_send.at[j], recv_sem=s2_recv.at[j],
            device_id={"dp": across}, device_id_type=MESH)

    def s3(layer, j):
        slot, index = 2 * layer + lax.rem(j, 2), layer * n + j
        return pltpu.make_async_remote_copy(
            src_ref=total.at[slot], dst_ref=g_hbm.at[index, :, half_of(core), :], send_sem=s3_send.at[slot], recv_sem=s3_recv.at[index],
            device_id={"dp": partner}, device_id_type=MESH)

    def put(layer, j):
        slot = 2 * layer + lax.rem(j, 2)
        return pltpu.make_async_copy(total.at[slot], g_hbm.at[layer * n + j, :, half_of(core), :], put_sem.at[slot])

    def free_total(layer, j):
        @pl.when(j >= 2)
        def _():
            s3(layer, j - 2).wait_send()
            put(layer, j - 2).wait()

    def deliver(layer, j, new, k):
        total[2 * layer + lax.rem(j, 2), k] = new
        wide = new.astype(F32)
        ssv[...] += jnp.sum((wide * wide).reshape(half // 8, 8, J), 0)

    def keep(j):
        return pltpu.make_async_copy(grad, own_hbm.at[j], own_sem)

    def step(t, _):
        p, j = t // n, lax.rem(t, n)

        @pl.when(jnp.logical_and(p == 1, j == 0))
        def _():
            keep(n - 1).wait()
            lax.fori_loop(0, blocks, to_layer_0, 0)
            get = pltpu.make_async_copy(x_hbm, h, x_sem.at[0])
            get.start()
            get.wait()

        @pl.when(jnp.logical_and(p == 2, j == 0))
        def _():
            to_across(dy_hbm, far_dy, 0).wait()
            to_across(h_hbm, far_h, 1).wait()
            get = pltpu.make_async_copy(far_h, h, x_sem.at[0])
            get.start()
            get_too = pltpu.make_async_copy(far_dy, dh, x_sem.at[1])
            get_too.start()
            get.wait()
            get_too.wait()

        @pl.when(j == 0)
        def _():
            lax.fori_loop(0, blocks, begin, 0)

        slot = next_weights(n + t)

        @pl.when(p == 2)
        def _():
            pltpu.make_async_copy(own_hbm.at[j], mine, own_sem).start()

        def block(r, _):
            here = rows(r)
            both = dot(a[here, :], wgu[slot])
            gate, up = both[:, :J], both[:, J:]
            by_act = dot_nt(dh[here, :], wd[slot]).astype(BF16).astype(F32)
            s = jax.nn.sigmoid(gate)
            silu = gate * s
            act[here, :] = (silu * up).astype(BF16)
            dgu[here, J:] = (by_act * silu).astype(BF16)
            dgu[here, :J] = (by_act * up * (s + silu * (1.0 - s))).astype(BF16)
            return 0

        lax.fori_loop(0, blocks, block, 0, unroll=True)

        @pl.when(jnp.logical_and(p == 0, j > 0))
        def _():
            keep(j - 1).wait()

        def rest(i, _):
            here = half_of(lax.rem(1 - core + i, 2))
            both = dot(at[here, :], dgu[...]).astype(BF16)
            grad[0, here, :] = both[:, :J]
            grad[1, here, :] = both[:, J:]
            grad[2, here, :] = dot(dht[here, :], act[...]).astype(BF16)

            @pl.when(jnp.logical_and(i == 0, p == 2))
            def _():
                pltpu.make_async_copy(own_hbm.at[j], mine, own_sem).wait()
                for k in range(3):
                    grad[k, here, :] = (grad[k, here, :].astype(F32) + mine[k, here, :].astype(F32)).astype(BF16)

            @pl.when(jnp.logical_and(i == 0, p >= 1))
            def _():
                s1(t - n).start()

            return 0

        lax.fori_loop(0, 2, rest, 0)

        @pl.when(p == 0)
        def _():
            keep(j).start()

            def back(r, _):
                acc[rows(r), :] += dot_nt(dgu[rows(r), :], wgu[slot])
                return 0

            lax.fori_loop(0, blocks, back, 0, unroll=True)

        @pl.when(p == 1)
        def _():
            s1(t - n).wait()
            for k in range(3):
                chip[j, k] = (grad[k, half_of(core), :].astype(F32) + near[lax.rem(t - n, 2), k].astype(F32)).astype(BF16)
            s2(j).start()

        @pl.when(p == 2)
        def _():
            free_total(1, j)
            s1(t - n).wait()
            for k in range(3):
                new = grad[k, half_of(core), :].astype(F32) + mine[k, half_of(core), :].astype(F32)
                deliver(1, j, (new + near[lax.rem(t - n, 2), k].astype(F32)).astype(BF16), k)
            s3(1, j).start()
            put(1, j).start()
            free_total(0, j)
            s2(j).wait()
            for k in range(3):
                deliver(0, j, (chip[j, k].astype(F32) + far[j, k].astype(F32)).astype(BF16), k)
            s3(0, j).start()
            put(0, j).start()

        return 0

    lax.fori_loop(0, 3 * n, step, 0)
    share = pltpu.make_async_remote_copy(
        src_ref=ssv, dst_ref=ssr, send_sem=ss_sem.at[0], recv_sem=ss_sem.at[1], device_id={"dp": partner}, device_id_type=MESH)
    share.start()
    for layer in range(2):
        for j in (n - 2, n - 1):
            s3(layer, j).wait_send()
            put(layer, j).wait()

    def arrived(j, _):
        s3(0, j).wait_recv()
        s3(1, j).wait_recv()
        return 0

    lax.fori_loop(0, n, arrived, 0)
    share.wait()
    ss_ref[...] = ssv[...] + ssr[...]


def call_gradients(x, dy, wg, wu, wd):
    tokens, d = x.shape
    n = wg.shape[2] // J
    half = d // 2
    hbm = pl.BlockSpec(memory_space=pl.ANY)
    dma = pltpu.SemaphoreType.DMA
    part = (3, half, J)
    out = pl.pallas_call(
        gradients,
        name="gradients",
        out_shape=(
            jax.ShapeDtypeStruct((2 * n, 3, d, J), BF16), jax.ShapeDtypeStruct((8, J), F32),
            *[jax.ShapeDtypeStruct((tokens, d), BF16)] * 3, jax.ShapeDtypeStruct((n, 3, d, J), BF16),
        ),
        in_specs=[hbm] * 5,
        out_specs=(hbm, pl.BlockSpec(memory_space=pltpu.VMEM), hbm, hbm, hbm, hbm),
        scratch_shapes=[
            pltpu.VMEM((tokens, d), BF16), pltpu.VMEM((tokens, d), BF16), pltpu.VMEM((d, tokens), BF16),
            pltpu.VMEM((tokens, d), BF16), pltpu.VMEM((d, tokens), BF16),
            pltpu.VMEM((tokens, d), F32),
            pltpu.VMEM((tokens, J), BF16), pltpu.VMEM((tokens, 2 * J), BF16),
            pltpu.VMEM((2, d, 2 * J), BF16), pltpu.VMEM((2, J, d), BF16),
            pltpu.VMEM((3, d, J), BF16), pltpu.VMEM((3, d, J), BF16), pltpu.VMEM((2, *part), BF16), pltpu.VMEM((n, *part), BF16),
            pltpu.VMEM((n, *part), BF16), pltpu.VMEM((4, *part), BF16),
            pltpu.VMEM((8, J), F32), pltpu.VMEM((8, J), F32),
            dma((3, 2)), dma((2,)), dma, dma((2,)), dma((2,)), dma, dma((2,)), dma((n,)), dma((n,)), dma((4,)), dma((2 * n,)), dma((4,)), dma((2,)),
        ],
        compiler_params=pltpu.CompilerParams(collective_id=0, has_side_effects=True, vmem_limit_bytes=VMEM_LIMIT),
    )(x, dy, wg, wu, wd)
    return out[0], out[1]


def adamw(count, ss, g, wg, wu, wd, mg, mu, md, vg, vu, vd, *outs):
    squares = jnp.sum(jnp.sum(ss[...], 0, keepdims=True), 1, keepdims=True)
    factor = jnp.minimum(1.0, 0.5 * lax.rsqrt(squares / count + 1e-30))
    for k, (w, m, v) in enumerate(((wg, mg, vg), (wu, mu, vu), (wd, md, vd))):
        mine = g[0, k].astype(F32)
        mine = (mine.T if k == 2 else mine) * factor
        new_m = 0.9 * m[0] + 0.1 * mine
        new_v = 0.95 * v[0] + 0.05 * mine * mine
        w_out, m_out, v_out = outs[k], outs[3 + k], outs[6 + k]
        old = w[0].astype(F32)
        w_out[0] = (old - 0.02 * (new_m * lax.rsqrt(new_v + 1e-8) + 0.1 * old)).astype(BF16)
        m_out[0] = new_m
        v_out[0] = new_v


def call_adamw(ss, g, weights, m, v):
    layers, d, ff = weights[0].shape
    n = ff // J
    wide = pl.BlockSpec((1, d, J), lambda l, j: (l, 0, j))
    tall = pl.BlockSpec((1, J, d), lambda l, j: (l, j, 0))
    three = [wide, wide, tall]
    count = float(3 * layers * d * ff)
    return pl.pallas_call(
        lambda *refs: adamw(count, *refs),
        name="adamw",
        grid=(layers, n),
        out_shape=[jax.ShapeDtypeStruct(w.shape, t) for t in (BF16, F32, F32) for w in weights],
        in_specs=[pl.BlockSpec((8, J), lambda l, j: (0, 0)), pl.BlockSpec((1, 3, d, J), lambda l, j: (l * n + j, 0, 0, 0))] + three * 3,
        out_specs=three * 3,
        compiler_params=pltpu.CompilerParams(vmem_limit_bytes=VMEM_LIMIT),
    )(ss, g, *weights, *m, *v)


def solution(mesh):
    def step(x, dy, *arrays):
        weights, m, v = (arrays[i : i + 3] for i in (0, 3, 6))
        g, ss = call_gradients(x[0], dy[0], *weights)
        return tuple(call_adamw(ss, g, weights, m, v))

    return jax.shard_map(
        step,
        mesh=mesh,
        in_specs=(P(("rep", "dp"), None, None),) * 2 + (P(None, None, None),) * 9,
        out_specs=(P("rep", None, None),) * 9,
        check_vma=False,
    )
```

time: 513 us -> 470 us (0.916)
  Pallas kernels: 512 us -> 469 us
    pallas_call x1, Pallas kernels: 399 us -> 357 us  [call_gradients(): pl.pallas_call(gradients, name='gradients', out_shape=(jax.ShapeDtypeStru...]
where the time goes in v2:
time: 470 us
  Pallas kernels  469 us (100%)
    pallas_call x1, Pallas kernels, call_gradients(): pl.pallas_call(gradients, name='gradients', out_shape=(jax.ShapeDtypeStru...  357 us
    pallas_call x1, Pallas kernels, call_adamw(): pl.pallas_call(lambda *refs: adamw(count, *refs), name='adamw', grid=(lay...  112 us

profile of v2, /device:TPU:0, one launch (start us, length us, event | category | flops | bytes accessed | tf_op | source)
XLA Modules:
  0.0 469.5 jit_solution(10867061606400641773)
XLA Ops:
  0.6 356.8 %gradients.1 = (bf16[20,3,1024,256]{3,2,1,0:T(8,128)(2,1)}, f32[8,256]{1,0:T(8,128)}, bf16[2048,1024]{1,0:T(8,128)(2,1)}, bf16[2048,1024]{1,0:T(8,128)(2,1)}, bf...) custom-call(bf16[2048,1024]{1,0:T(8,128)(2,1)} %bitcast.2, bf16[2048,1024]{1,0:T(8,128)(2,1)} %bitcast.3, ...), custom_call_target="tpu_custom_call" | custom-call | tf_op jit(solution)/shard_map/gradients/pallas_call | solution.py:300
  357.4 111.9 %adamw.1 = (bf16[2,1024,2560]{2,1,0:T(8,128)(2,1)}, bf16[2,1024,2560]{2,1,0:T(8,128)(2,1)}, bf16[2,2560,1024]{2,1,0:T(8,128)(2,1)}, f32[2,1024,2560]{2,1,0:T(8,1...) custom-call(f32[8,256]{1,0:T(8,128)} %get-tuple-element.11.refs_0_, ...), custom_call_target="tpu_custom_call" | custom-call | tf_op jit(solution)/shard_map/adamw/pallas_call | solution.py:347

commit v3 on v2

--- a/solution.py
+++ b/solution.py
@@ -9,6 +9,8 @@
 J = 256
 ROWS = 512
 VMEM_LIMIT = 67043328
+WIDE, TALL = 256, 64
+HANDED = 28 * 2**20
 MESH = pl.DeviceIdType.MESH
 
 
@@ -24,9 +26,9 @@
     return lax.rsqrt(jnp.mean(wide**2, -1, keepdims=True) + 1e-6)
 
 
-def gradients(x_hbm, dy_hbm, wg_hbm, wu_hbm, wd_hbm, g_hbm, ss_ref, h_hbm, far_h, far_dy, own_hbm, h, a, at, dh, dht, acc, act, dgu, wgu, wd,
-              grad, mine, near, chip, far, total, ssv, ssr, w_sem, x_sem, own_sem, far_send, far_recv, s1_send, s1_recv, s2_send, s2_recv,
-              s3_send, s3_recv, put_sem, ss_sem):
+def gradients(x_hbm, dy_hbm, wg_hbm, wu_hbm, wd_hbm, md_hbm, g_hbm, gd_hbm, ss_ref, h_hbm, far_h, far_dy, own_hbm, h, a, at, dh, dht, acc, act, dgu, wgu, wd,
+              grad, mine, near, chip, far, total, total_d, ssv, ssr, w_sem, x_sem, own_sem, far_send, far_recv, s1_send, s1_recv, s2_send, s2_recv,
+              s3_send, s3_recv, put_sem, ss_sem, hand_sem):
     tokens, d = h.shape
     blocks = tokens // ROWS
     n = wg_hbm.shape[2] // J
@@ -141,29 +143,63 @@
             src_ref=chip.at[j], dst_ref=far.at[j], send_sem=s2_send.at[j], recv_sem=s2_recv.at[j],
             device_id={"dp": across}, device_id_type=MESH)
 
+    def places(layer, j):
+        slot, index = 2 * layer + lax.rem(j, 2), layer * n + j
+        return [
+            (total.at[slot], g_hbm.at[index, :, half_of(core), :], slot, index),
+            (total_d.at[slot], gd_hbm.at[index, :, half_of(core)], 4 + slot, 2 * n + index),
+        ]
+
     def s3(layer, j):
-        slot, index = 2 * layer + lax.rem(j, 2), layer * n + j
-        return pltpu.make_async_remote_copy(
-            src_ref=total.at[slot], dst_ref=g_hbm.at[index, :, half_of(core), :], send_sem=s3_send.at[slot], recv_sem=s3_recv.at[index],
-            device_id={"dp": partner}, device_id_type=MESH)
+        return [
+            pltpu.make_async_remote_copy(
+                src_ref=src, dst_ref=dst, send_sem=s3_send.at[slot], recv_sem=s3_recv.at[index], device_id={"dp": partner}, device_id_type=MESH)
+            for src, dst, slot, index in places(layer, j)
+        ]
 
     def put(layer, j):
-        slot = 2 * layer + lax.rem(j, 2)
-        return pltpu.make_async_copy(total.at[slot], g_hbm.at[layer * n + j, :, half_of(core), :], put_sem.at[slot])
+        return [pltpu.make_async_copy(src, dst, put_sem.at[slot]) for src, dst, slot, _ in places(layer, j)]
+
+    def drained(layer, j):
+        for copy in s3(layer, j):
+            copy.wait_send()
+        for copy in put(layer, j):
+            copy.wait()
+
+    def leave(layer, j):
+        for copy in s3(layer, j) + put(layer, j):
+            copy.start()
 
     def free_total(layer, j):
         @pl.when(j >= 2)
         def _():
-            s3(layer, j - 2).wait_send()
-            put(layer, j - 2).wait()
+            drained(layer, j - 2)
 
     def deliver(layer, j, new, k):
-        total[2 * layer + lax.rem(j, 2), k] = new
         wide = new.astype(F32)
+        if k == 2:
+            total_d[2 * layer + lax.rem(j, 2)] = wide.T.astype(BF16)
+        else:
+            total[2 * layer + lax.rem(j, 2), k] = new
         ssv[...] += jnp.sum((wide * wide).reshape(half // 8, 8, J), 0)
 
     def keep(j):
         return pltpu.make_async_copy(grad, own_hbm.at[j], own_sem)
+
+    most, left, right = pl.ds(0, tokens), pl.ds(0, d), pl.ds(d, d)
+    hand = {
+        "acc": [(md_hbm.at[0, most, :], acc)],
+        "h": [(wd_hbm.at[1, most, :], h)],
+        "a": [(wd_hbm.at[0, most, :], a)],
+        "dh": [(wg_hbm.at[1, :, left], dh.at[left, :]), (wg_hbm.at[1, :, right], dh.at[right, :])],
+        "at": [(wg_hbm.at[0, :, most], at)],
+        "dht": [(wu_hbm.at[0, :, most], dht)],
+    }
+    hand = {name: [(*pair, k) for pair in pairs] for k, (name, pairs) in enumerate(hand.items())}
+    hand["dh"][1] = (*hand["dh"][1][:2], len(hand))
+
+    def handed(*names):
+        return [pltpu.make_async_copy(src, dst, hand_sem.at[k]) for name in names for src, dst, k in hand[name]]
 
     def step(t, _):
         p, j = t // n, lax.rem(t, n)
@@ -190,6 +226,11 @@
         @pl.when(j == 0)
         def _():
             lax.fori_loop(0, blocks, begin, 0)
+
+        @pl.when(jnp.logical_and(p == 2, j == 0))
+        def _():
+            for copy in handed("acc", "h"):
+                copy.start()
 
         slot = next_weights(n + t)
 
@@ -211,6 +252,11 @@
 
         lax.fori_loop(0, blocks, block, 0, unroll=True)
 
+        @pl.when(t == 3 * n - 1)
+        def _():
+            for copy in handed("a", "dh"):
+                copy.start()
+
         @pl.when(jnp.logical_and(p == 0, j > 0))
         def _():
             keep(j - 1).wait()
@@ -236,6 +282,11 @@
 
         lax.fori_loop(0, 2, rest, 0)
 
+        @pl.when(t == 3 * n - 1)
+        def _():
+            for copy in handed("at", "dht"):
+                copy.start()
+
         @pl.when(p == 0)
         def _():
             keep(j).start()
@@ -260,14 +311,12 @@
             for k in range(3):
                 new = grad[k, half_of(core), :].astype(F32) + mine[k, half_of(core), :].astype(F32)
                 deliver(1, j, (new + near[lax.rem(t - n, 2), k].astype(F32)).astype(BF16), k)
-            s3(1, j).start()
-            put(1, j).start()
+            leave(1, j)
             free_total(0, j)
             s2(j).wait()
             for k in range(3):
                 deliver(0, j, (chip[j, k].astype(F32) + far[j, k].astype(F32)).astype(BF16), k)
-            s3(0, j).start()
-            put(0, j).start()
+            leave(0, j)
 
         return 0
 
@@ -277,89 +326,147 @@
     share.start()
     for layer in range(2):
         for j in (n - 2, n - 1):
-            s3(layer, j).wait_send()
-            put(layer, j).wait()
+            drained(layer, j)
 
     def arrived(j, _):
-        s3(0, j).wait_recv()
-        s3(1, j).wait_recv()
+        for copy in s3(0, j) + s3(1, j):
+            copy.wait_recv()
         return 0
 
     lax.fori_loop(0, n, arrived, 0)
     share.wait()
+    for copy in handed(*hand):
+        copy.wait()
     ss_ref[...] = ssv[...] + ssr[...]
 
 
-def call_gradients(x, dy, wg, wu, wd):
+def call_gradients(x, dy, wg, wu, wd, md):
     tokens, d = x.shape
     n = wg.shape[2] // J
     half = d // 2
-    hbm = pl.BlockSpec(memory_space=pl.ANY)
+    hbm = pl.BlockSpec(memory_space=pltpu.HBM)
+    vmem = pl.BlockSpec(memory_space=pltpu.VMEM)
     dma = pltpu.SemaphoreType.DMA
     part = (3, half, J)
-    out = pl.pallas_call(
+    operands = [pltpu.with_memory_space_constraint(one, pltpu.HBM) for one in (x, dy, wg, wu, wd, md)]
+    g, gd, ss, _, _, _, _, *kept = pl.pallas_call(
         gradients,
         name="gradients",
         out_shape=(
-            jax.ShapeDtypeStruct((2 * n, 3, d, J), BF16), jax.ShapeDtypeStruct((8, J), F32),
-            *[jax.ShapeDtypeStruct((tokens, d), BF16)] * 3, jax.ShapeDtypeStruct((n, 3, d, J), BF16),
+            pltpu.HBM((2 * n, 2, d, J), BF16), pltpu.HBM((2 * n, J, d), BF16), jax.ShapeDtypeStruct((8, J), F32),
+            *[pltpu.HBM((tokens, d), BF16)] * 3, pltpu.HBM((n, 3, d, J), BF16),
+            pltpu.VMEM((tokens, d), BF16), pltpu.VMEM((tokens, d), BF16), pltpu.VMEM((d, tokens), BF16),
+            pltpu.VMEM((tokens, d), BF16), pltpu.VMEM((d, tokens), BF16), pltpu.VMEM((tokens, d), F32),
         ),
-        in_specs=[hbm] * 5,
-        out_specs=(hbm, pl.BlockSpec(memory_space=pltpu.VMEM), hbm, hbm, hbm, hbm),
+        in_specs=[hbm] * 6,
+        out_specs=(hbm, hbm, vmem, hbm, hbm, hbm, hbm, *[vmem] * 6),
         scratch_shapes=[
-            pltpu.VMEM((tokens, d), BF16), pltpu.VMEM((tokens, d), BF16), pltpu.VMEM((d, tokens), BF16),
-            pltpu.VMEM((tokens, d), BF16), pltpu.VMEM((d, tokens), BF16),
-            pltpu.VMEM((tokens, d), F32),
             pltpu.VMEM((tokens, J), BF16), pltpu.VMEM((tokens, 2 * J), BF16),
             pltpu.VMEM((2, d, 2 * J), BF16), pltpu.VMEM((2, J, d), BF16),
             pltpu.VMEM((3, d, J), BF16), pltpu.VMEM((3, d, J), BF16), pltpu.VMEM((2, *part), BF16), pltpu.VMEM((n, *part), BF16),
-            pltpu.VMEM((n, *part), BF16), pltpu.VMEM((4, *part), BF16),
+            pltpu.VMEM((n, *part), BF16), pltpu.VMEM((4, 2, half, J), BF16), pltpu.VMEM((4, J, half), BF16),
             pltpu.VMEM((8, J), F32), pltpu.VMEM((8, J), F32),
-            dma((3, 2)), dma((2,)), dma, dma((2,)), dma((2,)), dma, dma((2,)), dma((n,)), dma((n,)), dma((4,)), dma((2 * n,)), dma((4,)), dma((2,)),
+            dma((3, 2)), dma((2,)), dma, dma((2,)), dma((2,)), dma, dma((2,)), dma((n,)), dma((n,)), dma((8,)), dma((4 * n,)), dma((8,)), dma((2,)), dma((7,)),
         ],
-        compiler_params=pltpu.CompilerParams(collective_id=0, has_side_effects=True, vmem_limit_bytes=VMEM_LIMIT),
-    )(x, dy, wg, wu, wd)
-    return out[0], out[1]
-
-
-def adamw(count, ss, g, wg, wu, wd, mg, mu, md, vg, vu, vd, *outs):
+        compiler_params=pltpu.CompilerParams(collective_id=0, has_side_effects=True, vmem_limit_bytes=VMEM_LIMIT - HANDED),
+    )(*operands)
+    return (g, gd), ss, kept
+
+
+def adamw(count, near, ss, h, a, at, dh, dht, acc, g, gd, wg, wu, wd, mg, mu, md, vg, vu, vd, *outs):
+    d = wg.shape[1]
+    layer, j = pl.program_id(0), pl.program_id(1)
+    here = jnp.minimum(j, near - 1)
+    chunk = pl.ds(pl.multiple_of(here * J, J), J)
+    kept, first = j < near, layer == 0
     squares = jnp.sum(jnp.sum(ss[...], 0, keepdims=True), 1, keepdims=True)
     factor = jnp.minimum(1.0, 0.5 * lax.rsqrt(squares / count + 1e-30))
-    for k, (w, m, v) in enumerate(((wg, mg, vg), (wu, mu, vu), (wd, md, vd))):
-        mine = g[0, k].astype(F32)
-        mine = (mine.T if k == 2 else mine) * factor
-        new_m = 0.9 * m[0] + 0.1 * mine
-        new_v = 0.95 * v[0] + 0.05 * mine * mine
-        w_out, m_out, v_out = outs[k], outs[3 + k], outs[6 + k]
-        old = w[0].astype(F32)
-        w_out[0] = (old - 0.02 * (new_m * lax.rsqrt(new_v + 1e-8) + 0.1 * old)).astype(BF16)
-        m_out[0] = new_m
-        v_out[0] = new_v
-
-
-def call_adamw(ss, g, weights, m, v):
+
+    def take(k, size, w, m, v):
+        def some(i, _):
+            piece = pl.ds(pl.multiple_of(i * size, size), size)
+            mine = (gd[0, piece, :] if k == 2 else g[0, k, piece, :]).astype(F32) * factor
+            new_m = 0.9 * m(piece) + 0.1 * mine
+            new_v = 0.95 * v(piece) + 0.05 * mine * mine
+            old = w(piece).astype(F32)
+            outs[k][0, piece, :] = (old - 0.02 * (new_m * lax.rsqrt(new_v + 1e-8) + 0.1 * old)).astype(BF16)
+            outs[3 + k][0, piece, :] = new_m
+            outs[6 + k][0, piece, :] = new_v
+            return 0
+
+        lax.fori_loop(0, outs[k].shape[1] // size, some, 0, unroll=2)
+
+    def rows_of(ref):
+        return lambda piece: ref[0, piece, :]
+
+    def of_chunk(ref):
+        return lambda piece: ref[pl.ds(pl.multiple_of(here * J + piece.start, TALL), TALL), :]
+
+    gate, up, down = (rows_of(mg), rows_of(vg)), (rows_of(mu), rows_of(vu)), (rows_of(md), rows_of(vd))
+
+    @pl.when(jnp.logical_and(kept, first))
+    def _():
+        take(0, WIDE, lambda piece: at[piece, chunk], *gate)
+        take(1, WIDE, lambda piece: dht[piece, chunk], *up)
+        take(2, TALL, of_chunk(a), of_chunk(acc), down[1])
+
+    @pl.when(jnp.logical_and(kept, layer == 1))
+    def _():
+        across = d // J
+        cols = pl.ds(pl.multiple_of(here % across * J, J), J)
+        take(0, WIDE, lambda piece: dh[pl.ds(pl.multiple_of(here // across * d + piece.start, WIDE), WIDE), cols], *gate)
+        take(1, WIDE, rows_of(wu), *up)
+        take(2, TALL, of_chunk(h), *down)
+
+    @pl.when(j >= near)
+    def _():
+        take(0, WIDE, rows_of(wg), *gate)
+        take(1, WIDE, rows_of(wu), *up)
+        take(2, TALL, rows_of(wd), *down)
+
+
+def call_adamw(ss, kept, g, weights, m, v):
     layers, d, ff = weights[0].shape
     n = ff // J
-    wide = pl.BlockSpec((1, d, J), lambda l, j: (l, 0, j))
-    tall = pl.BlockSpec((1, J, d), lambda l, j: (l, j, 0))
-    three = [wide, wide, tall]
+    near = kept[0].shape[0] // J
+    vmem = pl.BlockSpec(memory_space=pltpu.VMEM)
+
+    def there(l, j):
+        return jnp.maximum(j, near)
+
+    def there_0(l, j):
+        return jnp.where(l == 0, jnp.maximum(j, near), j)
+
+    def own(l, j):
+        return j
+
+    def wide(at):
+        return pl.BlockSpec((1, d, J), lambda l, j: (l, 0, at(l, j)))
+
+    def tall(at):
+        return pl.BlockSpec((1, J, d), lambda l, j: (l, at(l, j), 0))
+
     count = float(3 * layers * d * ff)
+    three = [wide(own), wide(own), tall(own)]
+    kept = [pltpu.with_memory_space_constraint(one, pltpu.VMEM) for one in kept]
     return pl.pallas_call(
-        lambda *refs: adamw(count, *refs),
+        lambda *refs: adamw(count, near, *refs),
         name="adamw",
         grid=(layers, n),
         out_shape=[jax.ShapeDtypeStruct(w.shape, t) for t in (BF16, F32, F32) for w in weights],
-        in_specs=[pl.BlockSpec((8, J), lambda l, j: (0, 0)), pl.BlockSpec((1, 3, d, J), lambda l, j: (l * n + j, 0, 0, 0))] + three * 3,
+        in_specs=[pl.BlockSpec((8, J), lambda l, j: (0, 0)), *[vmem] * 6, pl.BlockSpec((1, 2, d, J), lambda l, j: (l * n + j, 0, 0, 0)),
+                  pl.BlockSpec((1, J, d), lambda l, j: (l * n + j, 0, 0)),
+                  wide(there), wide(there_0), tall(there), wide(own), wide(own), tall(there_0), *three],
         out_specs=three * 3,
-        compiler_params=pltpu.CompilerParams(vmem_limit_bytes=VMEM_LIMIT),
-    )(ss, g, *weights, *m, *v)
+        compiler_params=pltpu.CompilerParams(vmem_limit_bytes=VMEM_LIMIT - HANDED),
+    )(ss, *kept, *g, *weights, *m, *v)
 
 
 def solution(mesh):
     def step(x, dy, *arrays):
         weights, m, v = (arrays[i : i + 3] for i in (0, 3, 6))
-        g, ss = call_gradients(x[0], dy[0], *weights)
-        return tuple(call_adamw(ss, g, weights, m, v))
+        g, ss, kept = call_gradients(x[0], dy[0], *weights, m[2])
+        return tuple(call_adamw(ss, kept, g, weights, m, v))
 
     return jax.shard_map(
         step,

time: 470 us -> 464 us (0.987)
  Pallas kernels: 469 us -> 463 us
    pallas_call x2, Pallas kernels: 469 us -> 463 us  [the longest x1 357 us: call_gradients(): pl.pallas_call(gradients, name='gradients', out_shape=(pltpu.HBM((2 * n,...]
where the time goes in v3:
time: 464 us
  Pallas kernels  463 us (100%)
    pallas_call x1, Pallas kernels, call_gradients(): pl.pallas_call(gradients, name='gradients', out_shape=(pltpu.HBM((2 * n,...  357 us
    pallas_call x1, Pallas kernels, call_adamw(): pl.pallas_call(lambda *refs: adamw(count, near, *refs), name='adamw', gri...  106 us

profile of v3, /device:TPU:0, one launch (start us, length us, event | category | flops | bytes accessed | tf_op | source)
XLA Modules:
  0.0 464.1 jit_solution(10120852148974535711)
XLA Ops:
  0.6 357.1 %gradients.1 = (bf16[20,2,1024,256]{3,2,1,0:T(8,128)(2,1)}, bf16[20,256,1024]{2,1,0:T(8,128)(2,1)}, f32[8,256]{1,0:T(8,128)}, bf16[2048,1024]{1,0:T(8,128)(2,1)}...) custom-call(bf16[2048,1024]{1,0:T(8,128)(2,1)} %bitcast.2, ...), custom_call_target="tpu_custom_call" | custom-call | tf_op jit(solution)/shard_map/gradients/pallas_call | solution.py:352
  357.8 106.1 %adamw.1 = (bf16[2,1024,2560]{2,1,0:T(8,128)(2,1)}, bf16[2,1024,2560]{2,1,0:T(8,128)(2,1)}, bf16[2,2560,1024]{2,1,0:T(8,128)(2,1)}, f32[2,1024,2560]{2,1,0:T(8,1...) custom-call(f32[8,256]{1,0:T(8,128)} %get-tuple-element.18.refs_0_, ...), custom_call_target="tpu_custom_call" | custom-call | tf_op jit(solution)/shard_map/adamw/pallas_call | solution.py:452

commit v4 on v3

--- a/solution.py
+++ b/solution.py
@@ -138,9 +138,9 @@
             src_ref=grad.at[:, half_of(1 - core), :], dst_ref=near.at[slot],
             send_sem=s1_send, recv_sem=s1_recv.at[slot], device_id={"dp": partner}, device_id_type=MESH)
 
-    def s2(j):
+    def s2(j, k):
         return pltpu.make_async_remote_copy(
-            src_ref=chip.at[j], dst_ref=far.at[j], send_sem=s2_send.at[j], recv_sem=s2_recv.at[j],
+            src_ref=chip.at[j, k], dst_ref=far.at[j, k], send_sem=s2_send.at[j, k], recv_sem=s2_recv.at[j, k],
             device_id={"dp": across}, device_id_type=MESH)
 
     def places(layer, j):
@@ -166,9 +166,10 @@
         for copy in put(layer, j):
             copy.wait()
 
-    def leave(layer, j):
-        for copy in s3(layer, j) + put(layer, j):
-            copy.start()
+    def leave(layer, j, k):
+        if k > 0:
+            s3(layer, j)[k - 1].start()
+            put(layer, j)[k - 1].start()
 
     def free_total(layer, j):
         @pl.when(j >= 2)
@@ -188,7 +189,7 @@
 
     most, left, right = pl.ds(0, tokens), pl.ds(0, d), pl.ds(d, d)
     hand = {
-        "acc": [(md_hbm.at[0, most, :], acc)],
+        "acc": [(md_hbm.at[1, most, :], acc)],
         "h": [(wd_hbm.at[1, most, :], h)],
         "a": [(wd_hbm.at[0, most, :], a)],
         "dh": [(wg_hbm.at[1, :, left], dh.at[left, :]), (wg_hbm.at[1, :, right], dh.at[right, :])],
@@ -302,7 +303,7 @@
             s1(t - n).wait()
             for k in range(3):
                 chip[j, k] = (grad[k, half_of(core), :].astype(F32) + near[lax.rem(t - n, 2), k].astype(F32)).astype(BF16)
-            s2(j).start()
+                s2(j, k).start()
 
         @pl.when(p == 2)
         def _():
@@ -311,12 +312,12 @@
             for k in range(3):
                 new = grad[k, half_of(core), :].astype(F32) + mine[k, half_of(core), :].astype(F32)
                 deliver(1, j, (new + near[lax.rem(t - n, 2), k].astype(F32)).astype(BF16), k)
-            leave(1, j)
+                leave(1, j, k)
             free_total(0, j)
-            s2(j).wait()
             for k in range(3):
+                s2(j, k).wait()
                 deliver(0, j, (chip[j, k].astype(F32) + far[j, k].astype(F32)).astype(BF16), k)
-            leave(0, j)
+                leave(0, j, k)
 
         return 0
 
@@ -366,7 +367,7 @@
             pltpu.VMEM((3, d, J), BF16), pltpu.VMEM((3, d, J), BF16), pltpu.VMEM((2, *part), BF16), pltpu.VMEM((n, *part), BF16),
             pltpu.VMEM((n, *part), BF16), pltpu.VMEM((4, 2, half, J), BF16), pltpu.VMEM((4, J, half), BF16),
             pltpu.VMEM((8, J), F32), pltpu.VMEM((8, J), F32),
-            dma((3, 2)), dma((2,)), dma, dma((2,)), dma((2,)), dma, dma((2,)), dma((n,)), dma((n,)), dma((8,)), dma((4 * n,)), dma((8,)), dma((2,)), dma((7,)),
+            dma((3, 2)), dma((2,)), dma, dma((2,)), dma((2,)), dma, dma((2,)), dma((n, 3)), dma((n, 3)), dma((8,)), dma((4 * n,)), dma((8,)), dma((2,)), dma((7,)),
         ],
         compiler_params=pltpu.CompilerParams(collective_id=0, has_side_effects=True, vmem_limit_bytes=VMEM_LIMIT - HANDED),
     )(*operands)
@@ -374,7 +375,8 @@
 
 
 def adamw(count, near, ss, h, a, at, dh, dht, acc, g, gd, wg, wu, wd, mg, mu, md, vg, vu, vd, *outs):
-    d = wg.shape[1]
+    d = 2 * wg.shape[1]
+    row, row_d = pl.program_id(2) * wg.shape[1], pl.program_id(2) * wd.shape[1]
     layer, j = pl.program_id(0), pl.program_id(1)
     here = jnp.minimum(j, near - 1)
     chunk = pl.ds(pl.multiple_of(here * J, J), J)
@@ -399,24 +401,27 @@
     def rows_of(ref):
         return lambda piece: ref[0, piece, :]
 
+    def rows(piece):
+        return pl.ds(pl.multiple_of(row + piece.start, WIDE), WIDE)
+
     def of_chunk(ref):
-        return lambda piece: ref[pl.ds(pl.multiple_of(here * J + piece.start, TALL), TALL), :]
+        return lambda piece: ref[pl.ds(pl.multiple_of(here * J + row_d + piece.start, TALL), TALL), :]
 
     gate, up, down = (rows_of(mg), rows_of(vg)), (rows_of(mu), rows_of(vu)), (rows_of(md), rows_of(vd))
 
     @pl.when(jnp.logical_and(kept, first))
     def _():
-        take(0, WIDE, lambda piece: at[piece, chunk], *gate)
-        take(1, WIDE, lambda piece: dht[piece, chunk], *up)
-        take(2, TALL, of_chunk(a), of_chunk(acc), down[1])
+        take(0, WIDE, lambda piece: at[rows(piece), chunk], *gate)
+        take(1, WIDE, lambda piece: dht[rows(piece), chunk], *up)
+        take(2, TALL, of_chunk(a), *down)
 
     @pl.when(jnp.logical_and(kept, layer == 1))
     def _():
         across = d // J
         cols = pl.ds(pl.multiple_of(here % across * J, J), J)
-        take(0, WIDE, lambda piece: dh[pl.ds(pl.multiple_of(here // across * d + piece.start, WIDE), WIDE), cols], *gate)
+        take(0, WIDE, lambda piece: dh[pl.ds(pl.multiple_of(here // across * d + row + piece.start, WIDE), WIDE), cols], *gate)
         take(1, WIDE, rows_of(wu), *up)
-        take(2, TALL, of_chunk(h), *down)
+        take(2, TALL, of_chunk(h), of_chunk(acc), down[1])
 
     @pl.when(j >= near)
     def _():
@@ -437,29 +442,43 @@
     def there_0(l, j):
         return jnp.where(l == 0, jnp.maximum(j, near), j)
 
+    def there_1(l, j):
+        return jnp.where(l == 1, jnp.maximum(j, near), j)
+
     def own(l, j):
         return j
 
-    def wide(at):
-        return pl.BlockSpec((1, d, J), lambda l, j: (l, 0, at(l, j)))
-
-    def tall(at):
-        return pl.BlockSpec((1, J, d), lambda l, j: (l, at(l, j), 0))
+    def wide(at, mode=None):
+        return pl.BlockSpec((1, d // 2, J), lambda l, j, i: (l, jnp.where(at(l, j) == j, i, 0), at(l, j)), pipeline_mode=mode)
+
+    def tall(at, mode=None):
+        return pl.BlockSpec((1, J // 2, d), lambda l, j, i: (l, 2 * at(l, j) + jnp.where(at(l, j) == j, i, 0), 0), pipeline_mode=mode)
 
     count = float(3 * layers * d * ff)
-    three = [wide(own), wide(own), tall(own)]
+    mode, mode_out = pl.Buffered(4), pl.Buffered(2)
     kept = [pltpu.with_memory_space_constraint(one, pltpu.VMEM) for one in kept]
+    gs = [pl.BlockSpec((1, 2, d // 2, J), lambda l, j, i: (l * n + j, 0, i, 0), pipeline_mode=mode),
+          pl.BlockSpec((1, J // 2, d), lambda l, j, i: (l * n + j, i, 0), pipeline_mode=mode)]
+    hbm = pl.BlockSpec(memory_space=pltpu.HBM)
+
+    def kernel(ss, h, a, at, dh, dht, acc, *refs):
+        pltpu.emit_pipeline(
+            lambda *blocks: adamw(count, near, ss, h, a, at, dh, dht, acc, *blocks),
+            grid=(layers, n, 2),
+            in_specs=[*gs, wide(there), wide(there_0), tall(there), wide(own, mode), wide(own, mode), tall(there_1, mode),
+                      wide(own, mode), wide(own, mode), tall(own, mode)],
+            out_specs=[wide(own, mode_out), wide(own, mode_out), tall(own, mode_out)] * 3,
+        )(*refs)
+
+    arrays = [pltpu.with_memory_space_constraint(one, pltpu.HBM) for one in (*g, *weights, *m, *v)]
     return pl.pallas_call(
-        lambda *refs: adamw(count, near, *refs),
+        kernel,
         name="adamw",
-        grid=(layers, n),
-        out_shape=[jax.ShapeDtypeStruct(w.shape, t) for t in (BF16, F32, F32) for w in weights],
-        in_specs=[pl.BlockSpec((8, J), lambda l, j: (0, 0)), *[vmem] * 6, pl.BlockSpec((1, 2, d, J), lambda l, j: (l * n + j, 0, 0, 0)),
-                  pl.BlockSpec((1, J, d), lambda l, j: (l * n + j, 0, 0)),
-                  wide(there), wide(there_0), tall(there), wide(own), wide(own), tall(there_0), *three],
-        out_specs=three * 3,
+        out_shape=[pltpu.HBM(w.shape, t) for t in (BF16, F32, F32) for w in weights],
+        in_specs=[vmem] * 7 + [hbm] * len(arrays),
+        out_specs=[hbm] * 9,
         compiler_params=pltpu.CompilerParams(vmem_limit_bytes=VMEM_LIMIT - HANDED),
-    )(ss, *kept, *g, *weights, *m, *v)
+    )(ss, *kept, *arrays)
 
 
 def solution(mesh):

time: 464 us -> 461 us (level)
  no operation moved by 1% of the time
where the time goes in v4:
time: 461 us
  Pallas kernels  460 us (100%)
    pallas_call x1, Pallas kernels, call_gradients(): pl.pallas_call(gradients, name='gradients', out_shape=(pltpu.HBM((2 * n,...  356 us
    pallas_call x1, Pallas kernels, call_adamw(): pl.pallas_call(kernel, name='adamw', out_shape=[pltpu.HBM(w.shape, t) for...  104 us

profile of v4, /device:TPU:0, one launch (start us, length us, event | category | flops | bytes accessed | tf_op | source)
XLA Modules:
  0.0 460.6 jit_solution(14659207059569053319)
XLA Ops:
  0.6 356.4 %gradients.1 = (bf16[20,2,1024,256]{3,2,1,0:T(8,128)(2,1)}, bf16[20,256,1024]{2,1,0:T(8,128)(2,1)}, f32[8,256]{1,0:T(8,128)}, bf16[2048,1024]{1,0:T(8,128)(2,1)}...) custom-call(bf16[2048,1024]{1,0:T(8,128)(2,1)} %bitcast.2, ...), custom_call_target="tpu_custom_call" | custom-call | tf_op jit(solution)/shard_map/gradients/pallas_call | solution.py:353
  357.0 103.6 %adamw.1 = (bf16[2,1024,2560]{2,1,0:T(8,128)(2,1)}, bf16[2,1024,2560]{2,1,0:T(8,128)(2,1)}, bf16[2,2560,1024]{2,1,0:T(8,128)(2,1)}, f32[2,1024,2560]{2,1,0:T(8,1...) custom-call(f32[8,256]{1,0:T(8,128)} %get-tuple-element.18.ss, ...), custom_call_target="tpu_custom_call" | custom-call | tf_op jit(solution)/shard_map/adamw/pallas_call | solution.py:474

commit v5 on v4

--- a/solution.py
+++ b/solution.py
@@ -10,7 +10,7 @@
 ROWS = 512
 VMEM_LIMIT = 67043328
 WIDE, TALL = 256, 64
-HANDED = 28 * 2**20
+HANDED = 71 * 2**19
 MESH = pl.DeviceIdType.MESH
 
 
@@ -26,8 +26,8 @@
     return lax.rsqrt(jnp.mean(wide**2, -1, keepdims=True) + 1e-6)
 
 
-def gradients(x_hbm, dy_hbm, wg_hbm, wu_hbm, wd_hbm, md_hbm, g_hbm, gd_hbm, ss_ref, h_hbm, far_h, far_dy, own_hbm, h, a, at, dh, dht, acc, act, dgu, wgu, wd,
-              grad, mine, near, chip, far, total, total_d, ssv, ssr, w_sem, x_sem, own_sem, far_send, far_recv, s1_send, s1_recv, s2_send, s2_recv,
+def gradients(x_hbm, dy_hbm, wg_hbm, wu_hbm, wd_hbm, md_hbm, g_hbm, gd_hbm, ss_ref, h_hbm, far_h, far_dy, own_hbm, h, a, at, dh, dht, acc, chip, act, dgu, wgu, wd,
+              grad, mine, near, far, total, total_d, ssv, ssr, w_sem, x_sem, own_sem, far_send, far_recv, s1_send, s1_recv, s2_send, s2_recv,
               s3_send, s3_recv, put_sem, ss_sem, hand_sem):
     tokens, d = h.shape
     blocks = tokens // ROWS
@@ -199,6 +199,11 @@
     hand = {name: [(*pair, k) for pair in pairs] for k, (name, pairs) in enumerate(hand.items())}
     hand["dh"][1] = (*hand["dh"][1][:2], len(hand))
 
+    near_n = tokens // J
+    hand["chip"] = [
+        (wu_hbm.at[1, pl.ds(k * half, half), pl.ds(j * J, J)], chip.at[j, k], 7 + 2 * j + k) for j in range(near_n) for k in range(2)
+    ]
+
     def handed(*names):
         return [pltpu.make_async_copy(src, dst, hand_sem.at[k]) for name in names for src, dst, k in hand[name]]
 
@@ -285,7 +290,7 @@
 
         @pl.when(t == 3 * n - 1)
         def _():
-            for copy in handed("at", "dht"):
+            for copy in handed("at", "dht", "chip"):
                 copy.start()
 
         @pl.when(p == 0)
@@ -357,25 +362,25 @@
             pltpu.HBM((2 * n, 2, d, J), BF16), pltpu.HBM((2 * n, J, d), BF16), jax.ShapeDtypeStruct((8, J), F32),
             *[pltpu.HBM((tokens, d), BF16)] * 3, pltpu.HBM((n, 3, d, J), BF16),
             pltpu.VMEM((tokens, d), BF16), pltpu.VMEM((tokens, d), BF16), pltpu.VMEM((d, tokens), BF16),
-            pltpu.VMEM((tokens, d), BF16), pltpu.VMEM((d, tokens), BF16), pltpu.VMEM((tokens, d), F32),
+            pltpu.VMEM((tokens, d), BF16), pltpu.VMEM((d, tokens), BF16), pltpu.VMEM((tokens, d), F32), pltpu.VMEM((n, *part), BF16),
         ),
         in_specs=[hbm] * 6,
-        out_specs=(hbm, hbm, vmem, hbm, hbm, hbm, hbm, *[vmem] * 6),
+        out_specs=(hbm, hbm, vmem, hbm, hbm, hbm, hbm, *[vmem] * 7),
         scratch_shapes=[
             pltpu.VMEM((tokens, J), BF16), pltpu.VMEM((tokens, 2 * J), BF16),
             pltpu.VMEM((2, d, 2 * J), BF16), pltpu.VMEM((2, J, d), BF16),
-            pltpu.VMEM((3, d, J), BF16), pltpu.VMEM((3, d, J), BF16), pltpu.VMEM((2, *part), BF16), pltpu.VMEM((n, *part), BF16),
-            pltpu.VMEM((n, *part), BF16), pltpu.VMEM((4, 2, half, J), BF16), pltpu.VMEM((4, J, half), BF16),
+            pltpu.VMEM((3, d, J), BF16), pltpu.VMEM((3, d, J), BF16), pltpu.VMEM((2, *part), BF16), pltpu.VMEM((n, *part), BF16), pltpu.VMEM((4, 2, half, J), BF16), pltpu.VMEM((4, J, half), BF16),
             pltpu.VMEM((8, J), F32), pltpu.VMEM((8, J), F32),
-            dma((3, 2)), dma((2,)), dma, dma((2,)), dma((2,)), dma, dma((2,)), dma((n, 3)), dma((n, 3)), dma((8,)), dma((4 * n,)), dma((8,)), dma((2,)), dma((7,)),
+            dma((3, 2)), dma((2,)), dma, dma((2,)), dma((2,)), dma, dma((2,)), dma((n, 3)), dma((n, 3)), dma((8,)), dma((4 * n,)), dma((8,)), dma((2,)), dma((7 + 2 * (tokens // J),)),
         ],
         compiler_params=pltpu.CompilerParams(collective_id=0, has_side_effects=True, vmem_limit_bytes=VMEM_LIMIT - HANDED),
     )(*operands)
     return (g, gd), ss, kept
 
 
-def adamw(count, near, ss, h, a, at, dh, dht, acc, g, gd, wg, wu, wd, mg, mu, md, vg, vu, vd, *outs):
+def adamw(count, near, ss, h, a, at, dh, dht, acc, ups, g, gd, wg, wu, wd, mg, mu, md, vg, vu, vd, *outs):
     d = 2 * wg.shape[1]
+    part = pl.program_id(2)
     row, row_d = pl.program_id(2) * wg.shape[1], pl.program_id(2) * wd.shape[1]
     layer, j = pl.program_id(0), pl.program_id(1)
     here = jnp.minimum(j, near - 1)
@@ -420,7 +425,7 @@
         across = d // J
         cols = pl.ds(pl.multiple_of(here % across * J, J), J)
         take(0, WIDE, lambda piece: dh[pl.ds(pl.multiple_of(here // across * d + row + piece.start, WIDE), WIDE), cols], *gate)
-        take(1, WIDE, rows_of(wu), *up)
+        take(1, WIDE, lambda piece: ups[here, part, piece, :], *up)
         take(2, TALL, of_chunk(h), of_chunk(acc), down[1])
 
     @pl.when(j >= near)
@@ -438,9 +443,6 @@
 
     def there(l, j):
         return jnp.maximum(j, near)
-
-    def there_0(l, j):
-        return jnp.where(l == 0, jnp.maximum(j, near), j)
 
     def there_1(l, j):
         return jnp.where(l == 1, jnp.maximum(j, near), j)
@@ -461,11 +463,11 @@
           pl.BlockSpec((1, J // 2, d), lambda l, j, i: (l * n + j, i, 0), pipeline_mode=mode)]
     hbm = pl.BlockSpec(memory_space=pltpu.HBM)
 
-    def kernel(ss, h, a, at, dh, dht, acc, *refs):
+    def kernel(ss, h, a, at, dh, dht, acc, ups, *refs):
         pltpu.emit_pipeline(
-            lambda *blocks: adamw(count, near, ss, h, a, at, dh, dht, acc, *blocks),
+            lambda *blocks: adamw(count, near, ss, h, a, at, dh, dht, acc, ups, *blocks),
             grid=(layers, n, 2),
-            in_specs=[*gs, wide(there), wide(there_0), tall(there), wide(own, mode), wide(own, mode), tall(there_1, mode),
+            in_specs=[*gs, wide(there), wide(there), tall(there), wide(own, mode), wide(own, mode), tall(there_1, mode),
                       wide(own, mode), wide(own, mode), tall(own, mode)],
             out_specs=[wide(own, mode_out), wide(own, mode_out), tall(own, mode_out)] * 3,
         )(*refs)
@@ -475,7 +477,7 @@
         kernel,
         name="adamw",
         out_shape=[pltpu.HBM(w.shape, t) for t in (BF16, F32, F32) for w in weights],
-        in_specs=[vmem] * 7 + [hbm] * len(arrays),
+        in_specs=[vmem] * 8 + [hbm] * len(arrays),
         out_specs=[hbm] * 9,
         compiler_params=pltpu.CompilerParams(vmem_limit_bytes=VMEM_LIMIT - HANDED),
     )(ss, *kept, *arrays)

time: 461 us -> 459 us (level)
  no operation moved by 1% of the time
where the time goes in v5:
time: 459 us
  Pallas kernels  458 us (100%)
    pallas_call x1, Pallas kernels, call_gradients(): pl.pallas_call(gradients, name='gradients', out_shape=(pltpu.HBM((2 * n,...  357 us
    pallas_call x1, Pallas kernels, call_adamw(): pl.pallas_call(kernel, name='adamw', out_shape=[pltpu.HBM(w.shape, t) for...  102 us

profile of v5, /device:TPU:0, one launch (start us, length us, event | category | flops | bytes accessed | tf_op | source)
XLA Modules:
  0.0 458.8 jit_solution(17914245157461241451)
XLA Ops:
  0.6 356.5 %gradients.1 = (bf16[20,2,1024,256]{3,2,1,0:T(8,128)(2,1)}, bf16[20,256,1024]{2,1,0:T(8,128)(2,1)}, f32[8,256]{1,0:T(8,128)}, bf16[2048,1024]{1,0:T(8,128)(2,1)}...) custom-call(bf16[2048,1024]{1,0:T(8,128)(2,1)} %bitcast.2, ...), custom_call_target="tpu_custom_call" | custom-call | tf_op jit(solution)/shard_map/gradients/pallas_call | solution.py:358
  357.2 101.7 %adamw.1 = (bf16[2,1024,2560]{2,1,0:T(8,128)(2,1)}, bf16[2,1024,2560]{2,1,0:T(8,128)(2,1)}, bf16[2,2560,1024]{2,1,0:T(8,128)(2,1)}, f32[2,1024,2560]{2,1,0:T(8,1...) custom-call(f32[8,256]{1,0:T(8,128)} %get-tuple-element.19.ss, ...), custom_call_target="tpu_custom_call" | custom-call | tf_op jit(solution)/shard_map/adamw/pallas_call | solution.py:476
